TPU v7x, 32 devices: a whole 2x2x4 slice. The times are simulated.
32 devices in a mesh: dp: 16 (over z, x, core), section: 2 (over y).
Axes of the slice: x: 2, y: 2, z: 4, core: 2. Of those that a mesh axis runs over, the one named last changes fastest.
Arguments:
- samples: bfloat16 [128, 512], P('dp'), may hold values from -6 to 6
- targets: bfloat16 [128, 512], P('dp'), may hold values from -6 to 6
- jacobian_targets: bfloat16 [128, 128, 512], P('dp'), may hold values from -0.1796875 to 0.1796875
- directions: int32 [128, 128], P('dp'), may hold values from 0 to 511
- plan: int32 [16, 8], P('dp'), may hold values from 0 to 7, each once within a row
- weights: bfloat16 [2, 512, 8192], P('section'), may hold values from -1 to 1
Outputs:
- gradients: float32 [2, 512, 8192], P('section', 'dp')
Inputs may be any that keep to these rules, and one draw needn't show every extreme that they name: `plan`: each row is a permutation of 0 to 7.
All inputs are finite; a program needn't handle non-finite values.
Results may differ from a plain program's by a relative error of at most 0.0034.
Values may be sent and summed in bfloat16 or wider, within the bound.
A program may use at most 128 MiB of HBM per device.

v0:
```python
import jax
import jax.numpy as jnp
from jax import lax
from jax.sharding import PartitionSpec as P

MICRO = 4
BATCH = 1


jacobian_weight = 32.0


def partner(block, axis, distance):
    count = lax.axis_size(axis)
    route = []
    for low in range(count):
        high = low | 1 << distance
        if high != low and high < count:
            route += [(low, high), (high, low)]
    return lax.ppermute(block, axis, route)


def contract_rows(left, right):
    return lax.dot_general(
        left, right, (((0,), (0,)), ((), ())), preferred_element_type=jnp.float32
    )


def against_rows(left, right):
    return lax.dot_general(
        left, right, (((1,), (1,)), ((), ())), preferred_element_type=jnp.float32
    )


def encoder_parts(inputs, chosen_dirs, w_first):
    linear = jnp.dot(inputs, w_first, preferred_element_type=jnp.float32)
    squash = jax.nn.sigmoid(linear)
    first_slope = squash * (1.0 + linear * (1.0 - squash))
    second_slope = squash * (1.0 - squash) * (2.0 + linear * (1.0 - 2.0 * squash))
    picked = jnp.take(w_first, chosen_dirs, axis=0)
    return (linear, squash, first_slope, second_slope, picked)


def encoder_forward(encoded):
    linear, squash, first_slope, second_slope, picked = encoded
    hidden = (linear * squash).astype(jnp.bfloat16)
    tangent = (first_slope[:, None, :] * picked.astype(jnp.float32)).astype(jnp.bfloat16)
    return (hidden, tangent)


def encoder_backward(inputs, chosen_dirs, encoded, cotangent, cotangent_tangent, reduced):
    linear, squash, first_slope, second_slope, picked = encoded
    projected = jnp.sum(cotangent_tangent.astype(jnp.float32) * picked.astype(jnp.float32), axis=1)
    grad_pre = (cotangent.astype(jnp.float32) * first_slope + second_slope * projected).astype(
        jnp.bfloat16
    )
    grad_picked = (cotangent_tangent.astype(jnp.float32) * first_slope[:, None, :]).astype(
        jnp.bfloat16
    )
    columns = grad_pre.shape[1]
    onehot = (
        chosen_dirs.reshape(-1)[:, None] == jnp.arange(reduced, dtype=jnp.int32)[None, :]
    ).astype(jnp.bfloat16)
    return contract_rows(inputs, grad_pre) + contract_rows(onehot, grad_picked.reshape(-1, columns))


def shards(samples, targets, jacobian_targets, directions, plan, weights):
    section_index = lax.axis_index("section")
    weight = weights[0]
    reduced, columns = weight.shape
    order_row = plan[0]

    def batch_slots(micro_index):
        return lax.dynamic_slice_in_dim(order_row, micro_index * BATCH, BATCH)

    def encoder_rows(micro_index):
        chosen = batch_slots(micro_index)
        return (jnp.take(samples, chosen, axis=0), jnp.take(directions, chosen, axis=0))

    def decoder_rows(micro_index):
        chosen = batch_slots(micro_index)
        return (jnp.take(targets, chosen, axis=0), jnp.take(jacobian_targets, chosen, axis=0))

    half = columns // 2
    keep_part = lax.dynamic_slice_in_dim(weight, section_index * half, half, 1)
    give_part = lax.dynamic_slice_in_dim(weight, (1 - section_index) * half, half, 1)
    other_part = partner(give_part, "section", 0)
    w_first, w_last = lax.cond(
        section_index == 0, lambda: (keep_part, other_part), lambda: (other_part, keep_part)
    )
    cleared_half = jnp.zeros((reduced, half), jnp.float32)

    def advance(current, carried):
        first_total, last_total = carried
        inputs, chosen_dirs = encoder_rows(current)
        target_rows, jacobian_rows = decoder_rows(current)
        encoded = encoder_parts(inputs, chosen_dirs, w_first)
        hidden, tangent = encoder_forward(encoded)
        flattened = tangent.reshape(-1, half)
        output, jacobian = lax.psum(
            (against_rows(hidden, w_last), against_rows(flattened, w_last)), "section"
        )
        misfit = (output - target_rows.astype(jnp.float32)).astype(jnp.bfloat16)
        jac_misfit = (
            jacobian_weight * (jacobian - jacobian_rows.reshape(jacobian.shape).astype(jnp.float32))
        ).astype(jnp.bfloat16)
        grad_last = contract_rows(misfit, hidden) + contract_rows(jac_misfit, flattened)
        cotangent = jnp.dot(misfit, w_last, preferred_element_type=jnp.float32).astype(jnp.bfloat16)
        cotangent_tangent = jnp.dot(jac_misfit, w_last, preferred_element_type=jnp.float32).astype(
            jnp.bfloat16
        )
        cotangent_tangent = cotangent_tangent.reshape(tangent.shape)
        grad_first = encoder_backward(
            inputs, chosen_dirs, encoded, cotangent, cotangent_tangent, reduced
        )
        return (first_total + grad_first, last_total + grad_last)

    first_total, last_total = lax.fori_loop(0, MICRO, advance, (cleared_half, cleared_half))
    stacked = jnp.stack([first_total, last_total])
    row_sums = lax.psum_scatter(stacked, "dp", scatter_dimension=1, tiled=True)
    result = lax.all_to_all(row_sums, "section", split_axis=0, concat_axis=2, tiled=True)
    return result


def solution(mesh):
    placed = (
        P("dp", None),
        P("dp", None),
        P("dp", None, None),
        P("dp", None),
        P("dp", None),
        P("section", None, None),
    )
    return jax.shard_map(
        shards, mesh=mesh, in_specs=placed, out_specs=P("section", "dp", None), check_vma=False
    )
```

profile of v0, /device:TPU:9, one launch (start us, length us, event | category | flops | bytes accessed | tf_op | source)
XLA Modules:
  0.0 558.2 jit_solution(160840656481375822)
XLA Ops:
  7.4 7.9 %dynamic-slice_bitcast_fusion = (bf16[512,4096]{1,0:T(8,128)(2,1)}, bf16[512,4096]{1,0:T(8,128)(2,1)}) fusion(bf16[1,512,8192]{2,1,0:T(8,128)(2,1)} %param.17, s32[]{:T(128)S(6)} %select_n.137, s32[]{:T(128)S(6)} %select_n.136), kind=kLoop, calls=%fused_computation.48 | loop fusion | bytes 16777224 | tf_op jit(solution)/shard_map/dynamic_slice | solution.py:85
  15.2 1.2 collective-permute-start
  16.5 90.5 %collective-permute-done = bf16[512,4096]{1,0:T(8,128)(2,1)} collective-permute-done((bf16[512,4096]{1,0:T(8,128)(2,1)}, bf16[512,4096]{1,0:T(8,128)(2,1)}, u32[]{:S(2)}, u32[]{:S(2)}) %collective-permute-start) | collective-permute-done | bytes 4194336 | tf_op jit(solution)/shard_map/ppermute | solution.py:20
  107.0 6.9 %conditional.1 = (bf16[512,4096]{1,0:T(8,128)(2,1)S(1)}, bf16[512,4096]{1,0:T(8,128)(2,1)}) conditional(s32[]{:T(128)} %convert_element_type.116, (bf16[512,4096]{1,0:T(8,128)(2,1)}, bf16[512,4096]{1,0:T(8,128)(2,1)}) %tuple.26, (bf16[512,4096]{1,0:T(8,128)(2,1)}, bf16[512,4096]{1,0:T(8,128)(2,1)}) %tuple.27), branch_computations={%region_0.0_spmd, %region_1.0_spmd} | conditional | bytes 16777232 | solution.py:88
  107.0 2.2 copy.12
  109.2 4.7 copy.13
  113.9 1.9 copy-done
  115.8 230.2 %while.19 = (s32[]{:T(128)}, f32[512,4096]{1,0:T(8,128)}, f32[512,4096]{1,0:T(8,128)}, s32[8]{0:T(128)S(1)}, bf16[8,512]{1,0:T(8,128)(2,1)S(1)}, /*index=5*/bf16...) while((s32[]{:T(128)}, f32[512,4096]{1,0:T(8,128)}, ...), condition=%wide.region_6.8_spmd.clone, body=%wide.region_2.7_spmd.clone.sunk | while | flops 2186144512 | bytes 67948848 | solution.py:118
  115.8 0.6 dynamic_slice.26
  118.4 0.7 compare_and_fusion.2
  119.1 2.8 fusion.73
  122.0 4.9 gather_fusion
  126.9 4.4 fusion.75
  131.4 3.4 fusion.77
  134.8 3.8 psum.27
  138.5 0.7 fusion.78
  139.3 2.8 fusion.79
  142.1 13.3 %all-reduce.2.cloned.1.call-done = f32[128,512]{1,0:T(8,128)} async-done(((f32[128,512]{1,0:T(8,128)}), f32[128,512]{1,0:T(8,128)}) %all-reduce.2.cloned.1.call-update) | async-done | bytes 262160 | tf_op jit(solution)/shard_map/while/body/eval_jaxpr/psum | solution.py:100
  155.4 3.2 fusion.76
  158.6 5.0 select_add_fusion.4
  163.6 5.8 %select_add_fusion.5 = f32[512,4096]{1,0:T(8,128)} fusion(f32[512,4096]{1,0:T(8,128)} %get-tuple-element.387, f32[4096]{0:T(1024)S(1)} %get-tuple-element.364, f32[512]{0:T(512)S(1)} %convert.45, pred[]{:T(512)S(6)} %compare.6, f32[4096]{0:T(1024)S(1)} %get-tuple-element.359, bf16[128,4096]{1,0:T(8,128)(2,1)S(1)} %gather_fusion, ...), kind=kOutput, calls=%fused_computation.1.clone.1 | convolution fusion | flops 547684352 | bytes 18254976 | tf_op jit(solution)/shard_map/while/body/eval_jaxpr/dot_general | solution.py:24
  169.3 0.6 dynamic_slice.26
  171.9 0.7 compare_and_fusion.2
  172.6 2.8 fusion.73
  175.4 4.9 gather_fusion
  180.4 4.4 fusion.75
  184.9 3.4 fusion.77
  188.3 3.8 psum.27
  192.0 0.7 fusion.78
  192.8 2.9 fusion.79
  195.6 12.7 %all-reduce.2.cloned.1.call-done = f32[128,512]{1,0:T(8,128)} async-done(((f32[128,512]{1,0:T(8,128)}), f32[128,512]{1,0:T(8,128)}) %all-reduce.2.cloned.1.call-update) | async-done | bytes 262160 | tf_op jit(solution)/shard_map/while/body/eval_jaxpr/psum | solution.py:100
  208.3 3.2 fusion.76
  211.5 8.4 %select_add_fusion.4 = f32[512,4096]{1,0:T(8,128)} fusion(f32[512,4096]{1,0:T(8,128)} %get-tuple-element.386, f32[4096]{0:T(1024)S(1)} %fusion.80, f32[512]{0:T(512)S(1)} %convert.44, pred[]{:T(512)S(6)} %compare.6, f32[128,4096]{1,0:T(8,128)S(1)} %get-tuple-element.363, f32[4096]{0:T(1024)S(1)} %get-tuple-element.359, s32[128]{0:T(128)S(1)} %bitcast.85), kind=kOutput, calls=%fused_computation.2.clone.1 | convolution fusion | flops 546373632 | bytes 18909696 | tf_op jit(solution)/shard_map/while/body/eval_jaxpr/dot_general | solution.py:24
  219.9 8.3 %select_add_fusion.5 = f32[512,4096]{1,0:T(8,128)} fusion(f32[512,4096]{1,0:T(8,128)} %get-tuple-element.387, f32[4096]{0:T(1024)S(1)} %get-tuple-element.364, f32[512]{0:T(512)S(1)} %convert.45, pred[]{:T(512)S(6)} %compare.6, f32[4096]{0:T(1024)S(1)} %get-tuple-element.359, bf16[128,4096]{1,0:T(8,128)(2,1)S(1)} %gather_fusion, ...), kind=kOutput, calls=%fused_computation.1.clone.1 | convolution fusion | flops 547684352 | bytes 18254976 | tf_op jit(solution)/shard_map/while/body/eval_jaxpr/dot_general | solution.py:24
  228.2 0.6 dynamic_slice.26
  230.8 0.7 compare_and_fusion.2
  231.5 2.8 fusion.73
  234.4 4.9 gather_fusion
  239.3 4.4 fusion.75
  243.8 3.4 fusion.77
  247.2 3.8 psum.27
  251.0 0.7 fusion.78
  251.7 2.9 fusion.79
  254.5 12.7 %all-reduce.2.cloned.1.call-done = f32[128,512]{1,0:T(8,128)} async-done(((f32[128,512]{1,0:T(8,128)}), f32[128,512]{1,0:T(8,128)}) %all-reduce.2.cloned.1.call-update) | async-done | bytes 262160 | tf_op jit(solution)/shard_map/while/body/eval_jaxpr/psum | solution.py:100
  267.2 3.2 fusion.76
  270.4 8.4 %select_add_fusion.4 = f32[512,4096]{1,0:T(8,128)} fusion(f32[512,4096]{1,0:T(8,128)} %get-tuple-element.386, f32[4096]{0:T(1024)S(1)} %fusion.80, f32[512]{0:T(512)S(1)} %convert.44, pred[]{:T(512)S(6)} %compare.6, f32[128,4096]{1,0:T(8,128)S(1)} %get-tuple-element.363, f32[4096]{0:T(1024)S(1)} %get-tuple-element.359, s32[128]{0:T(128)S(1)} %bitcast.85), kind=kOutput, calls=%fused_computation.2.clone.1 | convolution fusion | flops 546373632 | bytes 18909696 | tf_op jit(solution)/shard_map/while/body/eval_jaxpr/dot_general | solution.py:24
  278.8 8.3 %select_add_fusion.5 = f32[512,4096]{1,0:T(8,128)} fusion(f32[512,4096]{1,0:T(8,128)} %get-tuple-element.387, f32[4096]{0:T(1024)S(1)} %get-tuple-element.364, f32[512]{0:T(512)S(1)} %convert.45, pred[]{:T(512)S(6)} %compare.6, f32[4096]{0:T(1024)S(1)} %get-tuple-element.359, bf16[128,4096]{1,0:T(8,128)(2,1)S(1)} %gather_fusion, ...), kind=kOutput, calls=%fused_computation.1.clone.1 | convolution fusion | flops 547684352 | bytes 18254976 | tf_op jit(solution)/shard_map/while/body/eval_jaxpr/dot_general | solution.py:24
  287.1 0.6 dynamic_slice.26
  289.7 0.7 compare_and_fusion.2
  290.4 2.8 fusion.73
  293.3 4.9 gather_fusion
  298.2 4.4 fusion.75
  302.7 3.4 fusion.77
  306.1 3.8 psum.27
  309.9 0.7 fusion.78
  310.6 2.9 fusion.79
  313.5 12.7 %all-reduce.2.cloned.1.call-done = f32[128,512]{1,0:T(8,128)} async-done(((f32[128,512]{1,0:T(8,128)}), f32[128,512]{1,0:T(8,128)}) %all-reduce.2.cloned.1.call-update) | async-done | bytes 262160 | tf_op jit(solution)/shard_map/while/body/eval_jaxpr/psum | solution.py:100
  326.2 3.2 fusion.76
  329.4 8.4 %select_add_fusion.4 = f32[512,4096]{1,0:T(8,128)} fusion(f32[512,4096]{1,0:T(8,128)} %get-tuple-element.386, f32[4096]{0:T(1024)S(1)} %fusion.80, f32[512]{0:T(512)S(1)} %convert.44, pred[]{:T(512)S(6)} %compare.6, f32[128,4096]{1,0:T(8,128)S(1)} %get-tuple-element.363, f32[4096]{0:T(1024)S(1)} %get-tuple-element.359, s32[128]{0:T(128)S(1)} %bitcast.85), kind=kOutput, calls=%fused_computation.2.clone.1 | convolution fusion | flops 546373632 | bytes 18909696 | tf_op jit(solution)/shard_map/while/body/eval_jaxpr/dot_general | solution.py:24
  337.7 8.3 %select_add_fusion.5 = f32[512,4096]{1,0:T(8,128)} fusion(f32[512,4096]{1,0:T(8,128)} %get-tuple-element.387, f32[4096]{0:T(1024)S(1)} %get-tuple-element.364, f32[512]{0:T(512)S(1)} %convert.45, pred[]{:T(512)S(6)} %compare.6, f32[4096]{0:T(1024)S(1)} %get-tuple-element.359, bf16[128,4096]{1,0:T(8,128)(2,1)S(1)} %gather_fusion, ...), kind=kOutput, calls=%fused_computation.1.clone.1 | convolution fusion | flops 547684352 | bytes 18254976 | tf_op jit(solution)/shard_map/while/body/eval_jaxpr/dot_general | solution.py:24
  346.1 11.6 %pad_maximum_fusion = f32[2,512,4096]{2,1,0:T(8,128)} fusion(f32[1,512,4096]{2,1,0:T(8,128)} %bitcast.4, f32[1,512,4096]{2,1,0:T(8,128)} %bitcast.80), kind=kLoop, calls=%fused_computation.47 | loop fusion | flops 4194304 | bytes 33554432 | tf_op jit(solution)/shard_map/stack | solution.py:119
  357.7 176.3 %reduce-scatter.2.cloned.1.call-done = f32[2,32,4096]{2,1,0:T(8,128)} async-done(((f32[2,512,4096]{2,1,0:T(8,128)}), f32[2,32,4096]{2,1,0:T(8,128)}) %reduce-scatter.2.cloned.1.call-update) | async-done | bytes 1048592 | tf_op jit(solution)/shard_map/reduce_scatter | solution.py:120
  533.9 16.1 %all_to_all.18 = f32[2,32,4096]{2,1,0:T(8,128)S(1)} all-to-all(f32[2,32,4096]{2,1,0:T(8,128)} %reduce-scatter.2.cloned.1.call-done), channel_id=1, replica_groups=mesh['dp'=16,'section'=2] {'section'}, dimensions={0} | all-to-all | bytes 2097152 | tf_op jit(solution)/shard_map/all_to_all | solution.py:121
  550.0 1.0 copy.8
  (57 shorter events, 0.6 us)
Async XLA Ops:
  15.2 91.8 %collective-permute-start = (bf16[512,4096]{1,0:T(8,128)(2,1)}, bf16[512,4096]{1,0:T(8,128)(2,1)}, u32[]{:S(2)}, u32[]{:S(2)}) collective-permute-start(bf16[512,4096]{1,0:T(8,128)(2,1)} %get-tuple-element.286), channel_id=1, source_target_pairs={{0,1},{1,0},{2,3},{3,2},{4,5},{5,4},{6,7},{7,6},{8,9},{9,8},{10,11... | collective-permute-start | bytes 12582920 | tf_op jit(solution)/shard_map/ppermute | solution.py:20
  107.0 8.8 %copy-start.2 = (bf16[8,512]{1,0:T(8,128)(2,1)S(1)}, bf16[8,512]{1,0:T(8,128)(2,1)}, u32[]{:S(2)}) copy-start(bf16[8,512]{1,0:T(8,128)(2,1)} %param.12) | copy-start | bytes 24580
  107.0 8.8 %copy-start.3 = (s32[1,8]{1,0:T(1,128)S(1)}, s32[1,8]{1,0:T(1,128)}, u32[]{:S(2)}) copy-start(s32[1,8]{1,0:T(1,128)} %param.16) | copy-start | bytes 100
  113.9 1.9 copy-start
  115.8 39.6 %all-reduce.2.cloned.1.call-start = ((), (), s32[]{:S(2)}) async-start(), calls=%async_computation.3 | async-start | bytes 524288 | tf_op jit(solution)/shard_map/while/body/eval_jaxpr/psum | solution.py:100
  158.6 5.0 copy-start.1
  169.3 39.0 %all-reduce.2.cloned.1.call-start = ((), (), s32[]{:S(2)}) async-start(), calls=%async_computation.3 | async-start | bytes 524288 | tf_op jit(solution)/shard_map/while/body/eval_jaxpr/psum | solution.py:100
  211.5 8.4 %copy-start.1 = (f32[128,512]{1,0:T(8,128)S(1)}, f32[128,512]{1,0:T(8,128)}, u32[]{:S(2)}) copy-start(f32[128,512]{1,0:T(8,128)} %all-reduce.2.cloned.1.call-done) | copy-start | bytes 786436 | tf_op jit(solution)/shard_map/while
  228.2 39.0 %all-reduce.2.cloned.1.call-start = ((), (), s32[]{:S(2)}) async-start(), calls=%async_computation.3 | async-start | bytes 524288 | tf_op jit(solution)/shard_map/while/body/eval_jaxpr/psum | solution.py:100
  270.4 8.4 %copy-start.1 = (f32[128,512]{1,0:T(8,128)S(1)}, f32[128,512]{1,0:T(8,128)}, u32[]{:S(2)}) copy-start(f32[128,512]{1,0:T(8,128)} %all-reduce.2.cloned.1.call-done) | copy-start | bytes 786436 | tf_op jit(solution)/shard_map/while
  287.1 39.0 %all-reduce.2.cloned.1.call-start = ((), (), s32[]{:S(2)}) async-start(), calls=%async_computation.3 | async-start | bytes 524288 | tf_op jit(solution)/shard_map/while/body/eval_jaxpr/psum | solution.py:100
  329.4 8.4 %copy-start.1 = (f32[128,512]{1,0:T(8,128)S(1)}, f32[128,512]{1,0:T(8,128)}, u32[]{:S(2)}) copy-start(f32[128,512]{1,0:T(8,128)} %all-reduce.2.cloned.1.call-done) | copy-start | bytes 786436 | tf_op jit(solution)/shard_map/while
  346.1 187.9 %reduce-scatter.2.cloned.1.call-start = ((), (), s32[]{:S(2)}) async-start(), calls=%async_computation.2 | async-start | bytes 17825792 | tf_op jit(solution)/shard_map/reduce_scatter | solution.py:120
Sparse Core Ops, SparseCore 0:
  131.5 23.8 all-reduce.1
  185.0 23.3 all-reduce.1
  243.9 23.3 all-reduce.1
  302.8 23.3 all-reduce.1
Sparse Core Ops, SparseCore 1:
  357.7 176.1 reduce-scatter.1
where the time goes:
time: 563 us; the launch traced here: 558 us
  waiting for transfers between devices  318 us (56%)
  matrix products  127 us (23%)
  local copies, waits for them, and re-layouts  39.8 us (7%)
  blocking collectives  31.2 us (6%)
  other arithmetic  17.6 us (3%)
  between operations  14.5 us (3%)
  loops' own time  8.12 us (1%)
    reduce_scatter x1, waiting for transfers between devices, shards(): row_sums = lax.psum_scatter(stacked, 'dp', scatter_dimension=1, tiled=True)  176 us
    ppermute x1, waiting for transfers between devices, partner(): return lax.ppermute(block, axis, route)  90.5 us
    dot_general x8, matrix products, contract_rows(): lax.dot_general(left, right, (((0,), (0,)), ((), ())), preferred_element_...  60.8 us
    psum x4, waiting for transfers between devices, advance(): lax.psum((against_rows(hidden, w_last), against_rows(flattened, w_last)),...  51.4 us
    dot_general x8, matrix products, against_rows(): lax.dot_general(left, right, (((1,), (1,)), ((), ())), preferred_element_...  31.2 us
    gather x4, local copies, waits for them, and re-layouts, encoder_parts(): picked = jnp.take(w_first, chosen_dirs, axis=0)  19.7 us
    all_to_all x1, blocking collectives, shards(): lax.all_to_all(row_sums, 'section', split_axis=0, concat_axis=2, tiled=True)  16.1 us
    psum x4, blocking collectives, advance(): lax.psum((against_rows(hidden, w_last), against_rows(flattened, w_last)),...  15.1 us
  transfers between devices with their start and end apart: 6, of which 6 were waited for; matrix products, arithmetic and copies ran while one was open for 5% of the time, Pallas kernels for 0%

commit v1 on v0

v1 whole, which is shorter than its diff:
```python
import functools

import jax
import jax.numpy as jnp
from jax import lax
from jax.experimental import pallas as pl
from jax.experimental.pallas import tpu as pltpu
from jax.sharding import PartitionSpec as P

MICRO = 4
GROUP = 4
PAD = 16

jacobian_weight = 32.0

VMEM = pl.BlockSpec(memory_space=pltpu.VMEM)
ANY = pl.BlockSpec(memory_space=pl.ANY)


def place():
    dp, sec = lax.axis_index("dp"), lax.axis_index("section")
    g = lax.rem(dp, GROUP)
    return dp, sec, g, dp - g


def greet(peers):
    barrier = pltpu.get_barrier_semaphore()
    for dp, sec in peers:
        pl.semaphore_signal(barrier, inc=1, device_id={"dp": dp, "section": sec})
    pl.semaphore_wait(barrier, len(peers))


def remote(src, dst, send, recv, dp, sec):
    return pltpu.make_async_remote_copy(
        src_ref=src, dst_ref=dst, send_sem=send, recv_sem=recv,
        device_id={"dp": dp, "section": sec},
    )


def spread_kernel(n_sec, pack, weight, packs, both, psend, precv, wsend, wrecv, local):
    dp, sec, g, base = place()
    cols = both.shape[2]
    near = [(base + lax.rem(g + k, GROUP), sec) for k in range(1, GROUP)]
    far = [(dp, lax.rem(sec + k, n_sec)) for k in range(1, n_sec)]
    greet(near + far)

    def part(section):
        start = pl.multiple_of((section * GROUP + g) * cols, cols)
        return weight.at[0, :, pl.ds(start, cols)]

    copies = [
        remote(part(s), both.at[sec], wsend.at[k], wrecv.at[k], d, s)
        for k, (d, s) in enumerate(far)
    ]
    copies += [
        remote(pack, packs.at[g], psend.at[k], precv.at[k], d, s)
        for k, (d, s) in enumerate(near)
    ]
    for copy in copies:
        copy.start()
    own = pltpu.make_async_copy(part(sec), both.at[sec], local)
    own.start()
    packs[g] = pack[...]
    own.wait()
    for copy in copies:
        copy.wait()


def forward_kernel(spt, dirs, xs, both, act, picked_out, slopes, partial):
    tangents = dirs.shape[1] // spt
    reduced = both.shape[1]
    rows = dirs.shape[1]
    lanes = lax.broadcasted_iota(jnp.int32, (rows, reduced), 1)
    onehot = (dirs[0] == lanes).astype(jnp.float32).astype(jnp.bfloat16)
    picked = jnp.dot(onehot, both[0], preferred_element_type=jnp.float32)
    picked_out[0] = picked.astype(jnp.bfloat16)
    linear = jnp.dot(xs[0], both[0], preferred_element_type=jnp.float32)
    squash = jax.nn.sigmoid(linear)
    first = squash * (1.0 + linear * (1.0 - squash))
    second = squash * (1.0 - squash) * (2.0 + linear * (1.0 - 2.0 * squash))
    slopes[0, 0:PAD] = first
    slopes[0, PAD : 2 * PAD] = second
    for i in range(spt):
        lo = i * tangents
        act[0, lo : lo + tangents] = (first[i : i + 1] * picked[lo : lo + tangents]).astype(
            jnp.bfloat16
        )
    act[0, rows:] = (linear * squash).astype(jnp.bfloat16)
    partial[0] = lax.dot_general(
        act[0], both[1], (((1,), (1,)), ((), ())), preferred_element_type=jnp.float32
    ).astype(jnp.bfloat16)


def misfit_kernel(
    n_sec, tangent_rows, partial, target, misfit,
    first_in, sums, second_in, s1, r1, s2, r2, s3, r3, s4, r4,
):
    dp, sec, g, base = place()
    half = GROUP // 2
    quads = n_sec * half
    core = lax.rem(g, 2)
    q = sec * half + g // 2
    partner = (base + (g // 2) * 2 + (1 - core), sec)

    def quad(k):
        other = lax.rem(q + k, quads)
        return other // half, lax.rem(other, half)

    def device(k):
        s, h = quad(k)
        return base + h * 2 + core, s

    def block(k, c):
        s, h = quad(k)
        return s * GROUP + h * 2 + c

    greet([partner] + [device(k) for k in range(1, quads)])
    order = list(range(1, quads)) + [0]
    across = [
        remote(partial.at[block(k, 1 - core)], first_in.at[k], s1.at[k], r1.at[k], *partner)
        for k in range(quads)
    ]
    for k in order:
        across[k].start()
    out = [None] + [
        remote(sums.at[k - 1], second_in.at[k - 1], s2.at[k - 1], r2.at[k - 1], *device(k))
        for k in range(1, quads)
    ]
    for k in range(1, quads):
        across[k].wait_recv()
        sums[k - 1] = (
            partial[block(k, core)].astype(jnp.float32) + first_in[k].astype(jnp.float32)
        ).astype(jnp.bfloat16)
        out[k].start()
    across[0].wait_recv()
    for k in range(quads):
        across[k].wait_send()
    mine = block(0, core)
    for k in range(1, quads):
        out[k].wait_recv()
    total = partial[mine].astype(jnp.float32) + first_in[0].astype(jnp.float32)
    for k in range(1, quads):
        total = total + second_in[k - 1].astype(jnp.float32)
    row = lax.broadcasted_iota(jnp.int32, total.shape, 0)
    gain = jnp.where(row < tangent_rows, jacobian_weight, 1.0)
    misfit[mine] = (gain * (total - target[...].astype(jnp.float32))).astype(jnp.bfloat16)
    for k in range(1, quads):
        out[k].wait_send()
    gather = [
        remote(misfit.at[mine], misfit.at[mine], s3.at[k - 1], r3.at[k - 1], *device(k))
        for k in range(1, quads)
    ]
    for copy in gather:
        copy.start()
    passed = [remote(misfit.at[mine], misfit.at[mine], s4.at[0], r4.at[0], *partner)]
    passed[0].start()
    for k in range(1, quads):
        gather[k - 1].wait_recv()
        came = block(quads - k, core)
        copy = remote(misfit.at[came], misfit.at[came], s4.at[k], r4.at[k], *partner)
        copy.start()
        passed.append(copy)
    for copy in gather:
        copy.wait_send()
    for copy in passed:
        copy.wait()


def backward_kernel(
    spt, dirs, xs, both, act, picked, slopes, misfit, grads, total, pulled, chosen
):
    step = pl.program_id(0)
    rows = dirs.shape[1]
    tangents = rows // spt
    reduced = both.shape[1]
    over_rows = (((0,), (0,)), ((), ()))

    @pl.when(step == 0)
    def _():
        total[...] = jnp.zeros_like(total)

    total[1] += lax.dot_general(
        misfit[0], act[0], over_rows, preferred_element_type=jnp.float32
    )
    cotangent = jnp.dot(misfit[0], both[1], preferred_element_type=jnp.float32).astype(jnp.bfloat16)
    first = slopes[0, 0:PAD]
    second = slopes[0, PAD : 2 * PAD]
    tail_row = lax.broadcasted_iota(jnp.int32, first.shape, 0)
    projected = jnp.zeros_like(first)
    for i in range(spt):
        lo = i * tangents
        part = cotangent[lo : lo + tangents].astype(jnp.float32)
        line = jnp.sum(
            part * picked[0, lo : lo + tangents].astype(jnp.float32), axis=0, keepdims=True
        )
        projected = jnp.where(tail_row == i, line, projected)
        pulled[lo : lo + tangents] = (part * first[i : i + 1]).astype(jnp.bfloat16)
    pulled[rows:] = (
        cotangent[rows:].astype(jnp.float32) * first + second * projected
    ).astype(jnp.bfloat16)
    lanes = lax.broadcasted_iota(jnp.int32, (rows, reduced), 1)
    chosen[:rows] = (dirs[0] == lanes).astype(jnp.float32).astype(jnp.bfloat16)
    chosen[rows:] = xs[0]
    total[0] += lax.dot_general(
        chosen[...], pulled[...], over_rows, preferred_element_type=jnp.float32
    )

    @pl.when(step == pl.num_programs(0) - 1)
    def _():
        grads[...] = total[...].astype(jnp.bfloat16)


def reduce_kernel(n_sec, n_s, grads, out, arrived, total, s1, r1, s2, r2, local):
    dp, sec, g, base = place()
    s = dp // GROUP
    team = n_sec * GROUP
    t = sec * GROUP + g
    _, rows, cols = grads.shape
    rows = rows // n_s
    own_rows = rows // GROUP

    def rows_of(owner):
        return pl.ds(pl.multiple_of(owner * rows, rows), rows)

    def mate(k):
        other = lax.rem(t + k, team)
        return other // GROUP, lax.rem(other, GROUP)

    peers = [lax.rem(s + k, n_s) for k in range(1, n_s)]
    mates = [mate(k) for k in range(1, team)]
    greet([(p * GROUP + g, sec) for p in peers] + [(base + h, l) for l, h in mates])
    sums = [
        remote(
            grads.at[:, rows_of(p), :], arrived.at[k], s1.at[k], r1.at[k], p * GROUP + g, sec
        )
        for k, p in enumerate(peers)
    ]
    for copy in sums:
        copy.start()
    for copy in sums:
        copy.wait_recv()
    for layer in range(n_sec):
        for h in range(GROUP):
            start = pl.multiple_of(s * rows + h * own_rows, own_rows)
            value = grads[layer, pl.ds(start, own_rows), :].astype(jnp.float32)
            for k in range(n_s - 1):
                value = value + arrived[k, layer, h * own_rows : (h + 1) * own_rows, :].astype(
                    jnp.float32
                )
            total[layer * GROUP + h] = value
    for copy in sums:
        copy.wait_send()
    columns = out.at[:, pl.ds(pl.multiple_of(t * cols, cols), cols)]
    hand = [
        remote(total.at[l * GROUP + h], columns, s2.at[k], r2.at[k], base + h, l)
        for k, (l, h) in enumerate(mates)
    ]
    for copy in hand:
        copy.start()
    keep = pltpu.make_async_copy(total.at[t], columns, local)
    keep.start()
    keep.wait()
    for copy in hand:
        copy.wait()


def shards(n_dp, n_sec, samples, targets, jacobian_targets, directions, plan, weights):
    sec = lax.axis_index("section")
    _, reduced, width = weights.shape
    tangents = directions.shape[1]
    team = n_sec * GROUP
    cols = width // team
    n_s = n_dp // GROUP
    spt = MICRO // n_sec
    rows = spt * tangents
    high = rows + PAD
    dma = lambda n: pltpu.SemaphoreType.DMA((n,))
    f32, bf16 = jnp.float32, jnp.bfloat16
    shape = jax.ShapeDtypeStruct
    limit = 56 * 1024 * 1024

    slots = plan[0, :MICRO]
    pack = jnp.concatenate(
        [
            jnp.take(samples, slots, axis=0).astype(f32),
            jnp.take(directions, slots, axis=0).astype(f32),
        ],
        axis=1,
    )
    pack = jnp.pad(pack, ((0, 8 - MICRO), (0, 0)))
    packs, both = pl.pallas_call(
        functools.partial(spread_kernel, n_sec),
        out_shape=(
            shape((GROUP,) + pack.shape, f32),
            shape((n_sec, reduced, cols), bf16),
        ),
        in_specs=[VMEM, ANY],
        out_specs=(VMEM, VMEM),
        scratch_shapes=[dma(GROUP - 1), dma(GROUP - 1), dma(n_sec - 1), dma(n_sec - 1),
                        pltpu.SemaphoreType.DMA],
        compiler_params=pltpu.CompilerParams(
            collective_id=0, has_side_effects=True, vmem_limit_bytes=limit
        ),
        name="spread",
    )(pack, weights)
    packs = packs[:, :MICRO].reshape(GROUP, n_sec, spt, -1).transpose(1, 0, 2, 3)
    packs = packs.reshape(team, spt, -1)
    xs = jnp.pad(packs[..., :reduced].astype(bf16), ((0, 0), (0, PAD - spt), (0, 0)))
    dirs = packs[..., reduced:].astype(jnp.int32).reshape(team, rows, 1)

    per = lambda *s: pl.BlockSpec((1,) + s, lambda i: (i,) + (0,) * len(s))
    all_of = lambda *s: pl.BlockSpec(s, lambda i: (0,) * len(s))
    common = [per(rows, 1), per(PAD, reduced), all_of(n_sec, reduced, cols)]
    act, picked, slopes, partial = pl.pallas_call(
        functools.partial(forward_kernel, spt),
        grid=(team,),
        out_shape=(
            shape((team, high, cols), bf16),
            shape((team, rows, cols), bf16),
            shape((team, 2 * PAD, cols), f32),
            shape((team, high, reduced), bf16),
        ),
        in_specs=common,
        out_specs=(per(high, cols), per(rows, cols), per(2 * PAD, cols), per(high, reduced)),
        compiler_params=pltpu.CompilerParams(vmem_limit_bytes=limit),
        name="forward",
    )(dirs, xs, both)

    own = lax.dynamic_slice_in_dim(slots, sec * spt, spt)
    target = jnp.concatenate(
        [
            jnp.take(jacobian_targets, own, axis=0).reshape(rows, reduced),
            jnp.pad(jnp.take(targets, own, axis=0), ((0, PAD - spt), (0, 0))),
        ]
    )
    quads = team // 2
    misfit = pl.pallas_call(
        functools.partial(misfit_kernel, n_sec, rows),
        out_shape=shape((team, high, reduced), bf16),
        in_specs=[VMEM, VMEM],
        out_specs=VMEM,
        scratch_shapes=[
            pltpu.VMEM((quads, high, reduced), bf16),
            pltpu.VMEM((quads - 1, high, reduced), bf16),
            pltpu.VMEM((quads - 1, high, reduced), bf16),
            dma(quads), dma(quads), dma(quads - 1), dma(quads - 1),
            dma(quads - 1), dma(quads - 1), dma(quads), dma(quads),
        ],
        compiler_params=pltpu.CompilerParams(
            collective_id=1, has_side_effects=True, vmem_limit_bytes=limit
        ),
        name="misfit",
    )(partial, target)

    grads = pl.pallas_call(
        functools.partial(backward_kernel, spt),
        grid=(team,),
        out_shape=shape((n_sec, reduced, cols), bf16),
        in_specs=common
        + [per(high, cols), per(rows, cols), per(2 * PAD, cols), per(high, reduced)],
        out_specs=all_of(n_sec, reduced, cols),
        scratch_shapes=[
            pltpu.VMEM((n_sec, reduced, cols), f32),
            pltpu.VMEM((high, cols), bf16),
            pltpu.VMEM((high, reduced), bf16),
        ],
        compiler_params=pltpu.CompilerParams(vmem_limit_bytes=limit),
        name="backward",
    )(dirs, xs, both, act, picked, slopes, misfit)

    own_rows = reduced // n_dp
    result = pl.pallas_call(
        functools.partial(reduce_kernel, n_sec, n_s),
        out_shape=shape((own_rows, width), f32),
        in_specs=[VMEM],
        out_specs=VMEM,
        scratch_shapes=[
            pltpu.VMEM((n_s - 1, n_sec, reduced // n_s, cols), bf16),
            pltpu.VMEM((team, own_rows, cols), f32),
            dma(n_s - 1), dma(n_s - 1), dma(team - 1), dma(team - 1),
            pltpu.SemaphoreType.DMA,
        ],
        compiler_params=pltpu.CompilerParams(
            collective_id=2, has_side_effects=True, vmem_limit_bytes=limit
        ),
        name="reduce",
    )(grads)
    return result[None]


def solution(mesh):
    placed = (
        P("dp", None),
        P("dp", None),
        P("dp", None, None),
        P("dp", None),
        P("dp", None),
        P("section", None, None),
    )
    body = functools.partial(shards, mesh.shape["dp"], mesh.shape["section"])
    return jax.shard_map(
        body, mesh=mesh, in_specs=placed, out_specs=P("section", "dp", None), check_vma=False
    )
```

time: 563 us -> 172 us (0.31)
  waiting for transfers between devices: 318 us -> 0 us
  Pallas kernels: 0 us -> 157 us
  matrix products: 127 us -> 0 us
  blocking collectives: 31.2 us -> 0 us
  local copies, waits for them, and re-layouts: 39.8 us -> 10.2 us
  between operations: 14.5 us -> 0.08 us
  other arithmetic: 17.6 us -> 4.55 us
  loops' own time: 8.12 us -> 0 us
    reduce_scatter x1 -> x0, waiting for transfers between devices: 176 us -> none  [shards(): row_sums = lax.psum_scatter(stacked, 'dp', scatter_dimension=1, tiled=True)]
    pallas_call x0 -> x5, Pallas kernels: none -> 157 us  [the longest x1 64.2 us: shards(): pl.pallas_call(functools.partial(reduce_kernel, n_sec, n_s), out_shape=sh...]
    dot_general x28 -> x0, matrix products: 127 us -> none  [the longest x8 60.8 us: contract_rows(): lax.dot_general(left, right, (((0,), (0,)), ((), ())), preferred_element_...]
    ppermute x1 -> x0, waiting for transfers between devices: 90.5 us -> none  [partner(): return lax.ppermute(block, axis, route)]
    psum x4 -> x0, waiting for transfers between devices: 51.4 us -> none  [advance(): lax.psum((against_rows(hidden, w_last), against_rows(flattened, w_last)),...]
    all_to_all x1 -> x0, blocking collectives: 16.1 us -> none  [shards(): lax.all_to_all(row_sums, 'section', split_axis=0, concat_axis=2, tiled=True)]
    gather x4, local copies, waits for them, and re-layouts: 19.7 us -> 4.33 us  [the longest x1 1.27 us: shards(): jnp.take(samples, slots, axis=0).astype(f32)]
    psum x4 -> x0, blocking collectives: 15.1 us -> none  [advance(): lax.psum((against_rows(hidden, w_last), against_rows(flattened, w_last)),...]
  transfers between devices with their start and end apart: 6 -> 0, of which waited for: 6 -> 0; matrix products, arithmetic and copies ran while one was open for 5% -> 0% of each run, Pallas kernels for 0% -> 0%
where the time goes in v1:
time: 172 us
  Pallas kernels  157 us (91%)
  local copies, waits for them, and re-layouts  10.2 us (6%)
  other arithmetic  4.55 us (3%)
    pallas_call x1, Pallas kernels, shards(): pl.pallas_call(functools.partial(reduce_kernel, n_sec, n_s), out_shape=sh...  64.2 us
    pallas_call x1, Pallas kernels, shards(): pl.pallas_call(functools.partial(misfit_kernel, n_sec, rows), out_shape=s...  36.2 us
    pallas_call x1, Pallas kernels, shards(): pl.pallas_call(functools.partial(spread_kernel, n_sec), out_shape=(shape(...  28.5 us
    pallas_call x1, Pallas kernels, shards(): pl.pallas_call(functools.partial(backward_kernel, spt), grid=(team,), out...  17.4 us
    pallas_call x1, Pallas kernels, shards(): pl.pallas_call(functools.partial(forward_kernel, spt), grid=(team,), out_...  10.5 us

profile of v1, /device:TPU:9, one launch (start us, length us, event | category | flops | bytes accessed | tf_op | source)
XLA Modules:
  0.0 171.6 jit_solution(14932033928499662156)
XLA Ops:
  0.0 0.0 copy-start
  0.0 0.8 compare_and_fusion
  0.8 0.7 fusion.3
  1.6 0.7 compare_and_fusion.1
  2.2 0.1 broadcast_bitcast_fusion
  2.3 0.7 fusion.2
  3.0 1.2 gather_fusion.1
  4.2 1.3 gather_fusion
  5.5 0.1 select_convert_fusion.1
  5.5 1.3 gather_fusion.3
  6.8 0.1 broadcast_select_fusion
  6.9 0.1 select_convert_fusion
  7.0 0.6 select_maximum_fusion.pack
  7.6 0.0 copy-done
  7.6 0.6 gather_fusion.2
  8.1 0.1 bitcast_select_fusion
  8.3 0.7 fusion.1.target
  9.0 28.5 %spread.1 = (f32[4,8,640]{2,1,0:T(8,128)}, bf16[2,512,1024]{2,1,0:T(8,128)(2,1)}) custom-call(f32[8,640]{1,0:T(8,128)} %select_maximum_fusion.pack, bf16[1,512,8192]{2,1,0:T(8,128)(2,1)} %weight.1), custom_call_target="tpu_custom_call" | custom-call | tf_op jit(solution)/shard_map/spread/pallas_call | solution.py:291
  37.5 0.9 slice.14
  38.5 0.7 pad.13.xs
  39.1 1.9 %reshape.116.dirs = s32[8,256,1]{2,1,0:T(8,128)} reshape(s32[8,2,128]{2,1,0:T(2,128)S(1)} %slice_convert_fusion.1) | data formatting | bytes 16384 | tf_op jit(solution)/shard_map/reshape | solution.py:309
  41.1 10.5 %forward.1 = (bf16[8,272,1024]{2,1,0:T(8,128)(2,1)}, bf16[8,256,1024]{2,1,0:T(8,128)(2,1)}, f32[8,32,1024]{2,1,0:T(8,128)}, bf16[8,272,512]{2,1,0:T(8,128)(2,1)}) custom-call(s32[8,256,1]{2,1,0:T(8,128)} %reshape.116.dirs, bf16[8,16,512]{2,1,0:T(8,128)(2,1)} %pad.13.xs, bf16[2,512,1024]{2,1,0:T(8,128)(2,1)} %get-tuple-element.12.both), custom_call_target="tpu_custom_call" | custom-call | tf_op jit(solution)/shard_map/forward/pallas_call | solution.py:314
  51.5 36.2 %misfit.1 = bf16[8,272,512]{2,1,0:T(8,128)(2,1)} custom-call(bf16[8,272,512]{2,1,0:T(8,128)(2,1)} %get-tuple-element.16.partial, bf16[272,512]{1,0:T(8,128)(2,1)} %fusion.1.target), custom_call_target="tpu_custom_call" | custom-call | tf_op jit(solution)/shard_map/misfit/pallas_call | solution.py:337
  87.8 17.4 %backward.1.grads = bf16[2,512,1024]{2,1,0:T(8,128)(2,1)} custom-call(s32[8,256,1]{2,1,0:T(8,128)} %reshape.116.dirs, bf16[8,16,512]{2,1,0:T(8,128)(2,1)} %pad.13.xs, bf16[2,512,1024]{2,1,0:T(8,128)(2,1)} %get-tuple-element.12.both, bf16[8,272,1024]{2,1,0:T(8,128)(2,1)} %get-tuple-element.13.act, bf16[8,256,1024]{2,1,0:T(8,128)(2,1)} %get-tuple-element.14.picked, ...), custom_call_target="tpu_custom_call" | custom-call | tf_op jit(solution)/shard_map/backward/pallas_call | solution.py:355
  105.1 64.2 %reduce.1 = f32[32,8192]{1,0:T(8,128)} custom-call(bf16[2,512,1024]{2,1,0:T(8,128)(2,1)} %backward.1.grads), custom_call_target="tpu_custom_call" | custom-call | tf_op jit(solution)/shard_map/reduce/pallas_call | solution.py:372
  169.4 2.3 %copy.11 = f32[1,32,8192]{2,1,0:T(8,128)} copy(f32[1,32,8192]{2,1,0:T(8,128)} %bitcast.21) | data formatting | bytes 2097152
  (6 shorter events, 0.1 us)
Async XLA Ops:
  0.0 7.6 %copy-start = (bf16[8,128,512]{2,1,0:T(8,128)(2,1)S(1)}, bf16[8,128,512]{2,1,0:T(8,128)(2,1)}, u32[]{:S(2)}) copy-start(bf16[8,128,512]{2,1,0:T(8,128)(2,1)} %param.8) | copy-start | bytes 3145732

commit v2 on v1

v2 whole, which is shorter than its diff:
```python
import functools

import jax
import jax.numpy as jnp
from jax import lax
from jax.experimental import pallas as pl
from jax.experimental.pallas import tpu as pltpu
from jax.sharding import PartitionSpec as P

MICRO = 4
GROUP = 4
PAD = 16
PIECES = 4

jacobian_weight = 32.0

VMEM = pl.BlockSpec(memory_space=pltpu.VMEM)
ANY = pl.BlockSpec(memory_space=pl.ANY)


def place():
    dp, sec = lax.axis_index("dp"), lax.axis_index("section")
    g = lax.rem(dp, GROUP)
    return dp, sec, g, dp - g


def greet(peers):
    barrier = pltpu.get_barrier_semaphore()
    for dp, sec in peers:
        pl.semaphore_signal(barrier, inc=1, device_id={"dp": dp, "section": sec})
    pl.semaphore_wait(barrier, len(peers))


def remote(src, dst, send, recv, dp, sec):
    return pltpu.make_async_remote_copy(
        src_ref=src, dst_ref=dst, send_sem=send, recv_sem=recv,
        device_id={"dp": dp, "section": sec},
    )


def spread_kernel(
    n_sec, n_s, plan, samples, directions, weight, packs, both,
    psend, precv, wsend, wrecv, zsend, zrecv, local,
):
    dp, sec, g, base = place()
    _, reduced, cols = both.shape
    parity = lax.rem(dp // GROUP, 2)
    twin = (dp + GROUP * (1 - 2 * parity), sec)
    near = [(base + lax.rem(g + k, GROUP), sec) for k in range(1, GROUP)]
    far = [(dp, lax.rem(sec + k, n_sec)) for k in range(1, n_sec)]
    greet(near + far + [twin])
    piece = reduced // 2 // PIECES

    def part(section):
        start = pl.multiple_of((section * GROUP + g) * cols, cols)
        return weight.at[0, :, pl.ds(start, cols)]

    def rows_of(c):
        return pl.ds(pl.multiple_of(parity * (reduced // 2) + c * piece, piece), piece)

    sent = []
    for c in range(PIECES):
        for k, (d, s) in enumerate(far):
            i = k * PIECES + c
            sent.append(
                remote(
                    part(s).at[rows_of(c)], both.at[sec, rows_of(c)],
                    wsend.at[i], wrecv.at[i], d, s,
                )
            )
    for copy in sent:
        copy.start()
    own = pltpu.make_async_copy(part(sec), both.at[sec], local)
    own.start()
    every = jnp.concatenate(
        [samples[...].astype(jnp.float32), directions[...].astype(jnp.float32)], axis=1
    )
    row = lax.broadcasted_iota(jnp.int32, every.shape, 0)
    packed = jnp.zeros_like(every)
    for k in range(MICRO):
        line = jnp.sum(jnp.where(row == plan[0, k], every, 0.0), axis=0, keepdims=True)
        packed = jnp.where(row == k, line, packed)
    packs[g] = packed
    own.wait()
    shared = [
        remote(packs.at[g], packs.at[g], psend.at[k], precv.at[k], d, s)
        for k, (d, s) in enumerate(near)
    ]
    for copy in shared:
        copy.start()
    passed = []
    for c in range(PIECES):
        for k in range(n_sec - 1):
            i = k * PIECES + c
            sent[c * (n_sec - 1) + k].wait_recv()
            came = both.at[lax.rem(sec + n_sec - 1 - k, n_sec), rows_of(c)]
            copy = remote(came, came, zsend.at[i], zrecv.at[i], *twin)
            copy.start()
            passed.append(copy)
    for copy in shared + passed:
        copy.wait()
    for copy in sent:
        copy.wait_send()


def onehot_columns(directions_row, reduced):
    rows = lax.broadcasted_iota(jnp.int32, (reduced, directions_row.shape[1]), 0)
    return (rows == directions_row.astype(jnp.int32)).astype(jnp.float32).astype(jnp.bfloat16)


def stack_rows(lines, shape):
    row = lax.broadcasted_iota(jnp.int32, shape, 0)
    result = jnp.zeros(shape, jnp.float32)
    for i, line in enumerate(lines):
        result = jnp.where(row == i, line, result)
    return result


def pack_row(packs, block, spt, i):
    return packs[lax.rem(block, GROUP), pl.ds(block // GROUP * spt + i, 1), :]


def forward_kernel(
    spt, plan, sec, packs, both, jac_target, targets,
    act, picked_out, slopes, partial, jac_out, target_out,
):
    block = pl.program_id(0)
    tangents, reduced = jac_target.shape[1:]
    rows = spt * tangents
    jac_out[...] = jac_target[...]

    @pl.when(block == 0)
    def _():
        all_targets = targets[...].astype(jnp.float32)
        row = lax.broadcasted_iota(jnp.int32, all_targets.shape, 0)
        lines = [
            jnp.sum(
                jnp.where(row == plan[0, sec[0] * spt + i], all_targets, 0.0),
                axis=0, keepdims=True,
            )
            for i in range(spt)
        ]
        target_out[...] = stack_rows(lines, target_out.shape).astype(jnp.bfloat16)

    packed = [pack_row(packs, block, spt, i) for i in range(spt)]
    xs = stack_rows([p[:, :reduced] for p in packed], (PAD, reduced)).astype(jnp.bfloat16)
    linear = jnp.dot(xs, both[0], preferred_element_type=jnp.float32)
    squash = jax.nn.sigmoid(linear)
    first = squash * (1.0 + linear * (1.0 - squash))
    second = squash * (1.0 - squash) * (2.0 + linear * (1.0 - 2.0 * squash))
    slopes[0, 0:PAD] = first
    slopes[0, PAD : 2 * PAD] = second
    for i in range(spt):
        lo = i * tangents
        picked = lax.dot_general(
            onehot_columns(packed[i][:, reduced:], reduced), both[0],
            (((0,), (0,)), ((), ())), preferred_element_type=jnp.float32,
        )
        picked_out[0, lo : lo + tangents] = picked.astype(jnp.bfloat16)
        act[0, lo : lo + tangents] = (first[i : i + 1] * picked).astype(jnp.bfloat16)
    act[0, rows:] = (linear * squash).astype(jnp.bfloat16)
    partial[0] = lax.dot_general(
        act[0], both[1], (((1,), (1,)), ((), ())), preferred_element_type=jnp.float32
    ).astype(jnp.bfloat16)


def step_kernel(
    n_sec, n_s, spt,
    partial, jac_target, target, packs, both, act_hbm, picked_hbm, slopes_hbm, out,
    first_in, sums, second_in, misfit, act, picked, slopes, total, grads,
    tails, xs_all, inbox, halves, finished,
    s1, r1, s2, r2, s3, r3, s4, r4, s5, r5, s6, r6, load, local,
):
    dp, sec, g, base = place()
    s = dp // GROUP
    half = GROUP // 2
    team = n_sec * GROUP
    quads = n_sec * half
    core = lax.rem(g, 2)
    q = sec * half + g // 2
    partner = (base + (g // 2) * 2 + (1 - core), sec)
    rows, reduced = spt * jac_target.shape[1], both.shape[1]
    tangents = rows // spt
    cols = both.shape[2]
    slab = reduced // n_s
    own_rows = slab // GROUP
    f32, bf16 = jnp.float32, jnp.bfloat16
    over_rows = (((0,), (0,)), ((), ()))

    def quad(k):
        other = lax.rem(q + k, quads)
        return other // half, lax.rem(other, half)

    def device(k):
        l, h = quad(k)
        return base + h * 2 + core, l

    def block(k, c):
        l, h = quad(k)
        return l * GROUP + h * 2 + c

    if n_s == 4:
        mate = s + 1 - 2 * lax.rem(s, 2)
        opposite = lax.rem(s + 2, 4)
        mate_opposite = lax.rem(mate + 2, 4)
        others = [mate, opposite]
    else:
        others = [lax.rem(s + k, n_s) for k in range(1, n_s)]
    team_peers = [
        ((base + lax.rem(g + k, GROUP)), lax.rem(sec + j, n_sec))
        for j in range(n_sec) for k in range(GROUP) if j or k
    ]
    greet(team_peers + [(o * GROUP + g, sec) for o in others])
    loads = [
        pltpu.make_async_copy(a, b, load.at[i])
        for i, (a, b) in enumerate(((act_hbm, act), (picked_hbm, picked), (slopes_hbm, slopes)))
    ]

    across = [
        remote(partial.at[block(k, 1 - core)], first_in.at[k], s1.at[k], r1.at[k], *partner)
        for k in range(quads)
    ]
    for k in list(range(1, quads)) + [0]:
        across[k].start()
    for copy in loads:
        copy.start()
    away = [None] + [
        remote(sums.at[k - 1], second_in.at[k - 1], s2.at[k - 1], r2.at[k - 1], *device(k))
        for k in range(1, quads)
    ]
    for k in range(1, quads):
        across[k].wait_recv()
        sums[k - 1] = (
            partial[block(k, core)].astype(f32) + first_in[k].astype(f32)
        ).astype(bf16)
        away[k].start()
    across[0].wait_recv()
    for k in range(quads):
        across[k].wait_send()
    mine = block(0, core)
    for k in range(1, quads):
        away[k].wait_recv()

    def whole(lo, hi):
        value = partial[mine, lo:hi].astype(f32) + first_in[0, lo:hi].astype(f32)
        for k in range(1, quads):
            value = value + second_in[k - 1, lo:hi].astype(f32)
        return value

    for i in range(spt):
        lo, hi = i * tangents, (i + 1) * tangents
        misfit[mine, lo:hi] = (
            jacobian_weight * (whole(lo, hi) - jac_target[i].astype(f32))
        ).astype(bf16)
    misfit[mine, rows:] = (whole(rows, rows + PAD) - target[...].astype(f32)).astype(bf16)
    for k in range(1, quads):
        away[k].wait_send()
    gather = [
        remote(misfit.at[mine], misfit.at[mine], s3.at[k - 1], r3.at[k - 1], *device(k))
        for k in range(1, quads)
    ]
    for copy in gather:
        copy.start()
    passed = [remote(misfit.at[mine], misfit.at[mine], s4.at[0], r4.at[0], *partner)]
    passed[0].start()
    for copy in loads:
        copy.wait()

    def last_of(b):
        total[1] += lax.dot_general(misfit[b], act[b], over_rows, preferred_element_type=f32)

    total[...] = jnp.zeros_like(total)
    last_of(mine)
    passed[0].wait_recv()
    last_of(block(0, 1 - core))
    for k in range(1, quads):
        gather[k - 1].wait_recv()
        came = block(quads - k, core)
        copy = remote(misfit.at[came], misfit.at[came], s4.at[k], r4.at[k], *partner)
        copy.start()
        passed.append(copy)
        last_of(came)
    for k in range(1, quads):
        passed[k].wait_recv()
        last_of(block(quads - k, 1 - core))

    def slab_of(owner):
        return pl.ds(pl.multiple_of(owner * slab, slab), slab)

    def link(layer, kind, source, to):
        i = layer * inbox.shape[1] + kind
        return remote(source, inbox.at[layer, kind], s5.at[i], r5.at[i], to * GROUP + g, sec)

    flights = {}

    def send_layer(layer):
        grads[layer] = total[layer].astype(bf16)
        if n_s == 4:
            flights[layer] = [
                link(layer, 0, grads.at[layer, slab_of(mate_opposite)], mate),
                link(layer, 1, grads.at[layer, slab_of(mate)], mate),
            ]
        else:
            flights[layer] = [
                link(layer, k, grads.at[layer, slab_of(o)], o) for k, o in enumerate(others)
            ]
        for copy in flights[layer]:
            copy.start()

    def relay(layer):
        if n_s == 4:
            flights[layer][0].wait_recv()
            halves[layer] = (
                grads[layer, slab_of(opposite), :].astype(f32) + inbox[layer, 0].astype(f32)
            ).astype(bf16)
            copy = link(layer, 2, halves.at[layer], opposite)
            copy.start()
            flights[layer].append(copy)

    columns = out.at[:, pl.ds(pl.multiple_of((sec * GROUP + g) * cols, cols), cols)]

    def hand(layer, k):
        h = lax.rem(g + k, GROUP)
        return remote(
            finished.at[layer * GROUP + h], columns,
            s6.at[layer * GROUP + k], r6.at[sec * GROUP + k], base + h, layer,
        )

    def keep():
        return pltpu.make_async_copy(finished.at[sec * GROUP + g], columns, local)

    def finish(layer):
        kinds = range(1, 3) if n_s == 4 else range(n_s - 1)
        for k in kinds:
            flights[layer][k].wait_recv()
        for h in range(GROUP):
            start = pl.multiple_of(s * slab + h * own_rows, own_rows)
            value = grads[layer, pl.ds(start, own_rows), :].astype(f32)
            for k in kinds:
                value = value + inbox[layer, k, h * own_rows : (h + 1) * own_rows].astype(f32)
            finished[layer * GROUP + h] = value
        for copy in flights[layer]:
            copy.wait_send()
        for k in range(1, GROUP):
            hand(layer, k).start()

        @pl.when(sec != layer)
        def _():
            hand(layer, 0).start()

        @pl.when(sec == layer)
        def _():
            keep().start()

    def pull(b, carry):
        cotangent = jnp.dot(misfit[b], both[1], preferred_element_type=f32)
        first = slopes[b, 0:PAD]
        second = slopes[b, PAD : 2 * PAD]
        lines = []
        chosen = []
        pulled = []
        packed = [pack_row(packs, b, spt, i) for i in range(spt)]
        for i in range(spt):
            lo = i * tangents
            part = cotangent[lo : lo + tangents]
            lines.append(
                jnp.sum(part * picked[b, lo : lo + tangents].astype(f32), axis=0, keepdims=True)
            )
            pulled.append((part * first[i : i + 1]).astype(bf16))
            chosen.append(onehot_columns(packed[i][:, reduced:], reduced))
        here = pl.ds(pl.multiple_of(b * PAD, PAD), PAD)
        tails[here, :] = (
            cotangent[rows:] * first + second * stack_rows(lines, first.shape)
        ).astype(bf16)
        xs_all[here, :] = stack_rows([p[:, :reduced] for p in packed], (PAD, reduced)).astype(bf16)
        total[0] += jnp.dot(
            jnp.concatenate(chosen, axis=1), jnp.concatenate(pulled, axis=0),
            preferred_element_type=f32,
        )
        return carry

    send_layer(1)
    lax.fori_loop(0, team // 2, pull, 0)
    relay(1)
    lax.fori_loop(team // 2, team, pull, 0)
    total[0] += lax.dot_general(
        xs_all[...], tails[...], over_rows, preferred_element_type=f32
    )
    send_layer(0)
    finish(1)
    relay(0)
    finish(0)

    for layer in range(n_sec):
        for k in range(1, GROUP):
            hand(layer, k).wait_send()

        @pl.when(sec != layer)
        def _():
            hand(layer, 0).wait_send()

    keep().wait()
    for j in range(n_sec):
        for k in range(GROUP):
            arrival = remote(
                finished.at[0], columns, s6.at[0], r6.at[j * GROUP + k], *partner
            )
            if k:
                arrival.wait_recv()
            else:

                @pl.when(sec != j)
                def _():
                    arrival.wait_recv()

    for copy in gather + passed:
        copy.wait_send()


def shards(n_dp, n_sec, samples, targets, jacobian_targets, directions, plan, weights):
    sec = lax.axis_index("section")
    _, reduced, width = weights.shape
    pool, tangents = directions.shape
    team = n_sec * GROUP
    cols = width // team
    n_s = n_dp // GROUP
    spt = MICRO // n_sec
    rows = spt * tangents
    high = rows + PAD
    dma = lambda n: pltpu.SemaphoreType.DMA((n,))
    f32, bf16 = jnp.float32, jnp.bfloat16
    shape = jax.ShapeDtypeStruct
    limit = 56 * 1024 * 1024

    links = (n_sec - 1) * PIECES
    packs, both = pl.pallas_call(
        functools.partial(spread_kernel, n_sec, n_s),
        out_shape=(
            shape((GROUP, pool, reduced + tangents), f32),
            shape((n_sec, reduced, cols), bf16),
        ),
        in_specs=[pl.BlockSpec(memory_space=pltpu.SMEM), VMEM, VMEM, ANY],
        out_specs=(VMEM, VMEM),
        scratch_shapes=[dma(GROUP - 1), dma(GROUP - 1), dma(links), dma(links),
                        dma(links), dma(links), pltpu.SemaphoreType.DMA],
        compiler_params=pltpu.CompilerParams(
            collective_id=0, has_side_effects=True, vmem_limit_bytes=limit
        ),
        name="spread",
    )(plan, samples, directions, weights)

    per = lambda *s: pl.BlockSpec((1,) + s, lambda i, *_: (i,) + (0,) * len(s))
    all_of = lambda *s: pl.BlockSpec(s, lambda i, *_: (0,) * len(s))
    sample = lambda i: jnp.minimum(i, spt - 1)
    act, picked, slopes, partial, jac_target, target = pl.pallas_call(
        functools.partial(forward_kernel, spt),
        out_shape=(
            shape((team, high, cols), bf16),
            shape((team, rows, cols), bf16),
            shape((team, 2 * PAD, cols), f32),
            shape((team, high, reduced), bf16),
            shape((spt, tangents, reduced), bf16),
            shape((PAD, reduced), bf16),
        ),
        grid_spec=pltpu.PrefetchScalarGridSpec(
            num_scalar_prefetch=2,
            grid=(team,),
            in_specs=[
                all_of(*packs.shape),
                all_of(*both.shape),
                pl.BlockSpec(
                    (1, tangents, reduced),
                    lambda i, plan, sec: (plan[0, sec[0] * spt + sample(i)], 0, 0),
                ),
                all_of(*targets.shape),
            ],
            out_specs=(
                per(high, cols), per(rows, cols), per(2 * PAD, cols), per(high, reduced),
                pl.BlockSpec((1, tangents, reduced), lambda i, *_: (sample(i), 0, 0)),
                all_of(PAD, reduced),
            ),
        ),
        compiler_params=pltpu.CompilerParams(vmem_limit_bytes=limit),
        name="forward",
    )(plan, sec.reshape(1), packs, both, jacobian_targets, targets)

    quads = team // 2
    kinds = 3 if n_s == 4 else n_s - 1
    slab = reduced // n_s
    vmem = pltpu.VMEM
    result = pl.pallas_call(
        functools.partial(step_kernel, n_sec, n_s, spt),
        out_shape=shape((reduced // n_dp, width), f32),
        in_specs=[VMEM] * 5 + [ANY] * 3,
        out_specs=VMEM,
        scratch_shapes=[
            vmem((quads, high, reduced), bf16),
            vmem((quads - 1, high, reduced), bf16),
            vmem((quads - 1, high, reduced), bf16),
            vmem((team, high, reduced), bf16),
            vmem(act.shape, bf16),
            vmem(picked.shape, bf16),
            vmem(slopes.shape, f32),
            vmem((n_sec, reduced, cols), f32),
            vmem((n_sec, reduced, cols), bf16),
            vmem((team * PAD, cols), bf16),
            vmem((team * PAD, reduced), bf16),
            vmem((n_sec, kinds, slab, cols), bf16),
            vmem((n_sec, slab, cols), bf16),
            vmem((team, reduced // n_dp, cols), f32),
            dma(quads), dma(quads), dma(quads - 1), dma(quads - 1),
            dma(quads - 1), dma(quads - 1), dma(quads), dma(quads),
            dma(n_sec * kinds), dma(n_sec * kinds), dma(team), dma(team),
            dma(3), pltpu.SemaphoreType.DMA,
        ],
        compiler_params=pltpu.CompilerParams(
            collective_id=1, has_side_effects=True, vmem_limit_bytes=limit
        ),
        name="step",
    )(partial, jac_target, target, packs, both, act, picked, slopes)
    return result[None]


def solution(mesh):
    placed = (
        P("dp", None),
        P("dp", None),
        P("dp", None, None),
        P("dp", None),
        P("dp", None),
        P("section", None, None),
    )
    body = functools.partial(shards, mesh.shape["dp"], mesh.shape["section"])
    return jax.shard_map(
        body, mesh=mesh, in_specs=placed, out_specs=P("section", "dp", None), check_vma=False
    )
```

time: 172 us -> 124 us (0.72)
  Pallas kernels: 157 us -> 121 us
  local copies, waits for them, and re-layouts: 10.2 us -> 2.26 us
  other arithmetic: 4.55 us -> 0 us
    pallas_call x5 -> x3, Pallas kernels: 157 us -> 121 us  [the longest x1 88.3 us: shards(): pl.pallas_call(functools.partial(step_kernel, n_sec, n_s, spt), out_shape...]
    gather x4 -> x0, local copies, waits for them, and re-layouts: 4.33 us -> none  [the longest x1 1.27 us: shards(): jnp.take(samples, slots, axis=0).astype(f32)]
    reshape x3 -> x0, local copies, waits for them, and re-layouts: 1.95 us -> none  [the longest x1 1.91 us: shards(): dirs = packs[..., reduced:].astype(jnp.int32).reshape(team, rows, 1)]
where the time goes in v2:
time: 124 us; the launch traced here: 123 us
  Pallas kernels  121 us (98%)
  local copies, waits for them, and re-layouts  2.26 us (2%)
    pallas_call x1, Pallas kernels, shards(): pl.pallas_call(functools.partial(step_kernel, n_sec, n_s, spt), out_shape...  88.3 us
    pallas_call x1, Pallas kernels, shards(): pl.pallas_call(functools.partial(spread_kernel, n_sec, n_s), out_shape=(s...  21.4 us
    pallas_call x1, Pallas kernels, shards(): pl.pallas_call(functools.partial(forward_kernel, spt), out_shape=(shape((...  11.2 us

profile of v2, /device:TPU:9, one launch (start us, length us, event | category | flops | bytes accessed | tf_op | source)
XLA Modules:
  0.0 123.2 jit_solution(10814785876123600494)
XLA Ops:
  0.0 21.4 %spread.1 = (f32[4,8,640]{2,1,0:T(8,128)}, bf16[2,512,1024]{2,1,0:T(8,128)(2,1)}) custom-call(s32[1,8]{1,0:T(1,128)} %plan.3, bf16[8,512]{1,0:T(8,128)(2,1)} %samples.1, s32[8,128]{1,0:T(8,128)} %directions.1, bf16[1,512,8192]{2,1,0:T(8,128)(2,1)} %weight.1), custom_call_target="tpu_custom_call" | custom-call | tf_op jit(solution)/shard_map/spread/pallas_call | solution.py:436
  21.4 11.2 %forward.1 = (bf16[8,272,1024]{2,1,0:T(8,128)(2,1)}, bf16[8,256,1024]{2,1,0:T(8,128)(2,1)}, f32[8,32,1024]{2,1,0:T(8,128)}, bf16[8,272,512]{2,1,0:T(8,128)(2,1)}...) custom-call(s32[1,8]{1,0:T(1,128)} %plan.3, s32[1]{0:T(128)} %bitcast.sec, f32[4,8,640]{2,1,0:T(8,128)} %get-tuple-element.13.packs, ...), custom_call_target="tpu_custom_call" | custom-call | tf_op jit(solution)/shard_map/forward/pallas_call | solution.py:455
  32.6 88.3 %step.1 = f32[32,8192]{1,0:T(8,128)} custom-call(bf16[8,272,512]{2,1,0:T(8,128)(2,1)} %get-tuple-element.15.partial, bf16[2,128,512]{2,1,0:T(8,128)(2,1)} %get-tuple-element.16.jac_target, bf16[16,512]{1,0:T(8,128)(2,1)} %get-tuple-element.17.target, f32[4,8,640]{2,1,0:T(8,128)} %get-tuple-element.13.packs, bf16[2,512,1024]{2,1,0:T(8,128)(2,1)} %get-tuple-element.14.both, ...), custom_call_target="tpu_custom_call" | custom-call | tf_op jit(solution)/shard_map/step/pallas_call | solution.py:491
  120.9 2.3 %copy.8 = f32[1,32,8192]{2,1,0:T(8,128)} copy(f32[1,32,8192]{2,1,0:T(8,128)} %bitcast.2) | data formatting | bytes 2097152
